TPU v7x, 32 devices: a whole 2x2x4 slice. The times are simulated.
32 devices in a mesh: grp: 2 (over x), tile: 16 (over z, y, core).
Axes of the slice: x: 2, y: 2, z: 4, core: 2. Of those that a mesh axis runs over, the one named last changes fastest.
Arguments:
- voltages: bfloat16 [2, 32, 128, 1024], P(None, ('grp', 'tile')), parts along dimension 1, may hold values from -6 to 6
Outputs:
- visibilities: float32 [2, 2, 136, 128, 128], P(None, 'grp', None, 'tile'), parts along dimension 1
There are 2 independent parts, one for each index of `grp`. A program takes and returns all parts, laid end to end along the dimension named above; each array names one. Nothing has to cross between parts.
All inputs are finite; a program needn't handle non-finite values.
Results may differ from a plain program's by a relative error of at most 0.0003.
Values may be sent and summed in bfloat16 or wider, within the bound.
No kernel may reach another device: no remote copies, remote signals or barrier semaphores. Data moves between devices by JAX's collectives and lax.ppermute only.
A program may use at most 64 MiB of HBM per device.

v0:
```python
import jax
import jax.numpy as jnp
import numpy as np
from jax import lax
from jax.sharding import PartitionSpec as P

NBLK = 16
TIME = 1024


def passed_along(block, axis, distance):
    devices = range(lax.axis_size(axis))
    route = [((i - distance) % len(devices), i) for i in devices]
    return lax.ppermute(block, axis, route)


def pair_tile(rows_side, cols_side):
    real_part = jnp.einsum(
        "cit,cjt->cij", rows_side[0], cols_side[0], preferred_element_type=jnp.float32
    ) + jnp.einsum("cit,cjt->cij", rows_side[1], cols_side[1], preferred_element_type=jnp.float32)
    imag_part = jnp.einsum(
        "cit,cjt->cij", rows_side[1], cols_side[0], preferred_element_type=jnp.float32
    ) - jnp.einsum("cit,cjt->cij", rows_side[0], cols_side[1], preferred_element_type=jnp.float32)
    return jnp.stack([real_part, imag_part]) / TIME


def covers_all(members, blocks_count):
    reached = set()
    for first_member in members:
        for second_member in members:
            reached.add((first_member - second_member) % blocks_count)
    return len(reached) == blocks_count


def search_cover(members, first_value, target_count, blocks_count):
    if len(members) == target_count:
        if covers_all(members, blocks_count):
            return members
        return []
    for candidate in range(first_value, blocks_count):
        outcome = search_cover(members + [candidate], candidate + 1, target_count, blocks_count)
        if outcome:
            return outcome
    return []


def cover_offsets(blocks_count):
    target_count = 2
    while target_count <= blocks_count:
        outcome = search_cover([0], 1, target_count, blocks_count)
        if outcome:
            return outcome
        target_count = target_count + 1
    return list(range(blocks_count))


def class_pair(members, distance, blocks_count):
    for first_member in members:
        for second_member in members:
            if (second_member - first_member) % blocks_count == distance:
                return (first_member, second_member)
    return (0, distance)


def cover_sources(stride, members):
    sources = []
    for row_block in range(NBLK):
        for col_block in range(row_block, NBLK):
            if row_block == col_block:
                sources.append(row_block * stride)
            else:
                gap_size = col_block - row_block
                distance = min(gap_size, NBLK - gap_size)
                first_member, second_member = class_pair(members, distance, NBLK)
                if gap_size == distance:
                    owner_block = (row_block - first_member) % NBLK
                else:
                    owner_block = (col_block - first_member) % NBLK
                sources.append(owner_block * stride + distance)
    return np.array(sources, np.int32)


def channel_order(received, slot_count, sources):
    rows_part = received.shape[4]
    width = received.shape[5]
    all_channels = received.shape[1] * received.shape[2] // NBLK
    arranged = received.reshape(2, NBLK, all_channels, slot_count, rows_part, width)
    arranged = jnp.transpose(arranged, (0, 2, 1, 3, 4, 5)).reshape(
        2, all_channels, NBLK * slot_count, rows_part, width
    )
    return jnp.take(arranged, jnp.asarray(sources), axis=2)


def on_device(voltages):
    split_count = lax.axis_size("tile") // NBLK
    own_block = lax.axis_index("tile") // split_count
    diagonal = pair_tile(voltages, voltages)
    members = cover_offsets(NBLK)
    fetched = {0: voltages}
    for member_offset in members[1:]:
        fetched[member_offset] = passed_along(voltages, "tile", -member_offset * split_count)
    tiles_list = [diagonal]
    for distance in range(1, NBLK // 2 + 1):
        first_member, second_member = class_pair(members, distance, NBLK)
        product = pair_tile(fetched[first_member], fetched[second_member])
        flipped = jnp.stack([jnp.swapaxes(product[0], 1, 2), -jnp.swapaxes(product[1], 1, 2)])
        first_block = (own_block + first_member) % NBLK
        second_block = (own_block + second_member) % NBLK
        tiles_list.append(jnp.where(first_block < second_block, product, flipped))
    tile_slots = jnp.stack(tiles_list, axis=2)
    received = lax.all_to_all(tile_slots[:, None], "tile", split_axis=4, concat_axis=1, tiled=True)
    return channel_order(received, NBLK // 2 + 1, cover_sources(NBLK // 2 + 1, members))


def solution(mesh):
    placed = (P(None, ("grp", "tile"), None, None),)
    return jax.shard_map(
        on_device,
        mesh=mesh,
        in_specs=placed,
        out_specs=P(None, "grp", None, "tile", None),
        check_vma=False,
    )
```

profile of v0, /device:TPU:15, one launch (start us, length us, event | category | flops | bytes accessed | tf_op | source)
XLA Modules:
  0.0 124.3 jit_solution(4143550448847985932)
XLA Ops:
  0.9 4.3 %collective-permute-start.2 = (bf16[2,1,128,1024]{3,2,1,0:T(8,128)(2,1)}, bf16[2,1,128,1024]{3,2,1,0:T(8,128)(2,1)}, u32[]{:S(2)}, u32[]{:S(2)}) collective-permute-start(bf16[2,1,128,1024]{3,2,1,0:T(8,128)(2,1)} %param.2), channel_id=1, source_target_pairs={{5,0},{6,1},{7,2},{8,3},{9,4},{10,5},{11,6},{12,7},{13,8},{14,9},{... | collective-permute-start | bytes 1572872 | tf_op jit(solution)/shard_map/ppermute | solution.py:14
  5.2 1.3 %fusion.32 = f32[128,128]{1,0:T(8,128)S(1)} fusion(bf16[2,1,128,1024]{3,2,1,0:T(8,128)(2,1)} %param.2), kind=kOutput, calls=%fused_computation.60 | convolution fusion | flops 33554432 | bytes 327680 | tf_op jit(solution)/shard_map/cit,cjt->cij/dot_general | solution.py:18
  6.5 1.3 %fusion.1 = f32[1,1,1,128,128]{4,3,2,1,0:T(8,128)S(1)} fusion(f32[128,128]{1,0:T(8,128)S(1)} %fusion.32, bf16[2,1,128,1024]{3,2,1,0:T(8,128)(2,1)} %param.2), kind=kOutput, calls=%fused_computation.21 | convolution fusion | flops 33570816 | bytes 393216 | tf_op jit(solution)/shard_map/cit,cjt->cij/dot_general | solution.py:20
  7.9 1.3 %fusion.15 = f32[128,128]{1,0:T(8,128)S(1)} fusion(bf16[2,1,128,1024]{3,2,1,0:T(8,128)(2,1)} %param.2), kind=kOutput, calls=%fused_computation.43 | convolution fusion | flops 33554432 | bytes 589824 | tf_op jit(solution)/shard_map/cit,cjt->cij/dot_general | solution.py:21
  9.4 5.8 %collective-permute-done = bf16[2,1,128,1024]{3,2,1,0:T(8,128)(2,1)S(1)} collective-permute-done((bf16[2,1,128,1024]{3,2,1,0:T(8,128)(2,1)}, bf16[2,1,128,1024]{3,2,1,0:T(8,128)(2,1)S(1)}, u32[]{:S(2)}, u32[]{:S(2)}) %collective-permute-start) | collective-permute-done | bytes 524320 | tf_op jit(solution)/shard_map/ppermute | solution.py:14
  16.3 2.3 %collective-permute-done.1 = bf16[2,1,128,1024]{3,2,1,0:T(8,128)(2,1)S(1)} collective-permute-done((bf16[2,1,128,1024]{3,2,1,0:T(8,128)(2,1)}, bf16[2,1,128,1024]{3,2,1,0:T(8,128)(2,1)S(1)}, u32[]{:S(2)}, u32[]{:S(2)}) %collective-permute-start.1) | collective-permute-done | bytes 524320 | tf_op jit(solution)/shard_map/ppermute | solution.py:14
  19.7 19.2 %collective-permute-done.2 = bf16[2,1,128,1024]{3,2,1,0:T(8,128)(2,1)} collective-permute-done((bf16[2,1,128,1024]{3,2,1,0:T(8,128)(2,1)}, bf16[2,1,128,1024]{3,2,1,0:T(8,128)(2,1)}, u32[]{:S(2)}, u32[]{:S(2)}) %collective-permute-start.2) | collective-permute-done | bytes 524320 | tf_op jit(solution)/shard_map/ppermute | solution.py:14
  40.1 1.2 fusion.50
  41.3 1.2 convolution_add_fusion.5
  42.5 1.2 convolution_subtract_fusion.5
  43.8 1.2 fusion.48
  45.0 1.2 fusion.46
  46.2 1.2 convolution_add_fusion.4
  47.4 1.2 convolution_subtract_fusion.4
  48.7 1.2 fusion.6
  51.1 1.2 convolution_add_fusion.3
  52.3 1.2 convolution_subtract_fusion.3
  53.7 1.3 %fusion.51 = f32[128,128]{0,1:T(8,128)S(1)} fusion(bf16[2,1,128,1024]{3,2,1,0:T(8,128)(2,1)} %copy-done.3, bf16[2,1,128,1024]{3,2,1,0:T(8,128)(2,1)} %collective-permute-done.3), kind=kOutput, calls=%fused_computation.102 | convolution fusion | flops 33554432 | bytes 589824 | tf_op jit(solution)/shard_map/cit,cjt->cij/dot_general | solution.py:20
  55.0 1.2 fusion.49
  56.2 1.2 convolution_add_fusion.2
  57.4 1.2 convolution_subtract_fusion.2
  58.7 1.2 fusion.47
  59.9 1.2 fusion.45
  61.1 1.2 convolution_add_fusion.1
  62.3 1.2 convolution_subtract_fusion.1
  63.7 1.3 %fusion.3 = f32[128,128]{1,0:T(8,128)S(1)} fusion(bf16[2,1,128,1024]{3,2,1,0:T(8,128)(2,1)} %collective-permute-done.3, bf16[2,1,128,1024]{3,2,1,0:T(8,128)(2,1)} %param.2), kind=kOutput, calls=%fused_computation.31 | convolution fusion | flops 33554432 | bytes 589824 | tf_op jit(solution)/shard_map/cit,cjt->cij/dot_general | solution.py:20
  65.0 1.2 fusion.18
  66.2 1.2 convolution_add_fusion
  67.4 1.2 convolution_subtract_fusion
  68.9 2.0 %copy.171 = f32[2,1,1,9,128,128]{5,0,3,2,1,4:T(2,128)} copy(f32[2,1,1,9,128,128]{5,4,3,0,2,1:T(8,128)S(1)} %bitcast.255) | data formatting | bytes 2359296 | tf_op jit(solution)/shard_map/broadcast_in_dim | solution.py:111
  70.9 23.7 %all-to-all-start = ((f32[2,1,1,9,128,128]{5,0,3,2,1,4:T(2,128)}), f32[2,1,1,9,128,128]{5,0,3,2,1,4:T(2,128)S(1)}, u32[]{:S(2)}, u32[]{:S(2)}) async-start(f32[2,1,1,9,128,128]{5,0,3,2,1,4:T(2,128)} %copy.171), calls=%async_computation | async-start | bytes 2359296 | tf_op jit(solution)/shard_map/all_to_all | solution.py:111
  94.6 27.7 %all-to-all-done = f32[2,1,1,9,128,128]{5,0,3,2,1,4:T(2,128)S(1)} async-done(((f32[2,1,1,9,128,128]{5,0,3,2,1,4:T(2,128)}), f32[2,1,1,9,128,128]{5,0,3,2,1,4:T(2,128)S(1)}, u32[]{:S(2)}, u32[]{:S(2)}) %all-to-all-start) | async-done | bytes 1179680 | tf_op jit(solution)/shard_map/all_to_all | solution.py:111
  (71 shorter events, 8.5 us)
Async XLA Ops:
  0.0 9.1 %copy-start.1 = (bf16[2,1,128,1024]{3,2,1,0:T(8,128)(2,1)S(1)}, bf16[2,1,128,1024]{3,2,1,0:T(8,128)(2,1)}, u32[]{:S(2)}) copy-start(bf16[2,1,128,1024]{3,2,1,0:T(8,128)(2,1)} %param.2) | copy-start | bytes 1572868
  0.0 15.2 %collective-permute-start = (bf16[2,1,128,1024]{3,2,1,0:T(8,128)(2,1)}, bf16[2,1,128,1024]{3,2,1,0:T(8,128)(2,1)S(1)}, u32[]{:S(2)}, u32[]{:S(2)}) collective-permute-start(bf16[2,1,128,1024]{3,2,1,0:T(8,128)(2,1)} %param.2), channel_id=1, source_target_pairs={{1,0},{2,1},{3,2},{4,3},{5,4},{6,5},{7,6},{8,7},{9,8},{10,9},{11,1... | collective-permute-start | bytes 1572872 | tf_op jit(solution)/shard_map/ppermute | solution.py:14
  0.7 17.9 %collective-permute-start.1 = (bf16[2,1,128,1024]{3,2,1,0:T(8,128)(2,1)}, bf16[2,1,128,1024]{3,2,1,0:T(8,128)(2,1)S(1)}, u32[]{:S(2)}, u32[]{:S(2)}) collective-permute-start(bf16[2,1,128,1024]{3,2,1,0:T(8,128)(2,1)} %param.2), channel_id=1, source_target_pairs={{2,0},{3,1},{4,2},{5,3},{6,4},{7,5},{8,6},{9,7},{10,8},{11,9},{12,... | collective-permute-start | bytes 1572872 | tf_op jit(solution)/shard_map/ppermute | solution.py:14
  0.9 38.0 %collective-permute-start.2 = (bf16[2,1,128,1024]{3,2,1,0:T(8,128)(2,1)}, bf16[2,1,128,1024]{3,2,1,0:T(8,128)(2,1)}, u32[]{:S(2)}, u32[]{:S(2)}) collective-permute-start(bf16[2,1,128,1024]{3,2,1,0:T(8,128)(2,1)} %param.2), channel_id=1, source_target_pairs={{5,0},{6,1},{7,2},{8,3},{9,4},{10,5},{11,6},{12,7},{13,8},{14,9},{... | collective-permute-start | bytes 1572872 | tf_op jit(solution)/shard_map/ppermute | solution.py:14
  5.2 48.4 %collective-permute-start.3 = (bf16[2,1,128,1024]{3,2,1,0:T(8,128)(2,1)}, bf16[2,1,128,1024]{3,2,1,0:T(8,128)(2,1)}, u32[]{:S(2)}, u32[]{:S(2)}) collective-permute-start(bf16[2,1,128,1024]{3,2,1,0:T(8,128)(2,1)} %param.2), channel_id=1, source_target_pairs={{8,0},{9,1},{10,2},{11,3},{12,4},{13,5},{14,6},{15,7},{0,8},{1,9},... | collective-permute-start | bytes 1572872 | tf_op jit(solution)/shard_map/ppermute | solution.py:14
  18.6 23.9 %copy-start.3 = (bf16[2,1,128,1024]{3,2,1,0:T(8,128)(2,1)}, bf16[2,1,128,1024]{3,2,1,0:T(8,128)(2,1)S(1)}, u32[]{:S(2)}) copy-start(bf16[2,1,128,1024]{3,2,1,0:T(8,128)(2,1)S(1)} %collective-permute-done.1) | copy-start | bytes 1572868
  53.6 1.4 %copy-start.4 = (bf16[2,1,128,1024]{3,2,1,0:T(8,128)(2,1)S(1)}, bf16[2,1,128,1024]{3,2,1,0:T(8,128)(2,1)}, u32[]{:S(2)}) copy-start(bf16[2,1,128,1024]{3,2,1,0:T(8,128)(2,1)} %copy-done.3) | copy-start | bytes 1572868
  63.6 1.4 %copy-start.2 = (bf16[2,1,128,1024]{3,2,1,0:T(8,128)(2,1)S(1)}, bf16[2,1,128,1024]{3,2,1,0:T(8,128)(2,1)}, u32[]{:S(2)}) copy-start(bf16[2,1,128,1024]{3,2,1,0:T(8,128)(2,1)} %param.2) | copy-start | bytes 1572868
  70.9 23.7 %copy-start = (s32[136]{0:T(256)S(1)}, s32[136]{0:T(256)}, u32[]{:S(2)}) copy-start(s32[136]{0:T(256)} %constant.111) | copy-start | bytes 1636
  70.9 51.4 %all-to-all-start = ((f32[2,1,1,9,128,128]{5,0,3,2,1,4:T(2,128)}), f32[2,1,1,9,128,128]{5,0,3,2,1,4:T(2,128)S(1)}, u32[]{:S(2)}, u32[]{:S(2)}) async-start(f32[2,1,1,9,128,128]{5,0,3,2,1,4:T(2,128)} %copy.171), calls=%async_computation | async-start | bytes 2359296 | tf_op jit(solution)/shard_map/all_to_all | solution.py:111
where the time goes:
time: 125 us; the launch traced here: 124 us
  waiting for transfers between devices  55 us (44%)
  matrix products  34.5 us (28%)
  starting transfers between devices  28.9 us (23%)
  local copies, waits for them, and re-layouts  4.71 us (4%)
    all_to_all x1, waiting for transfers between devices, on_device(): lax.all_to_all(tile_slots[:, None], 'tile', split_axis=4, concat_axis=1,...  27.7 us
    ppermute x4, waiting for transfers between devices, passed_along(): return lax.ppermute(block, axis, route)  27.3 us
    all_to_all x1, starting transfers between devices, on_device(): lax.all_to_all(tile_slots[:, None], 'tile', split_axis=4, concat_axis=1,...  23.7 us
    dot_general x9, matrix products, pair_tile(): jnp.einsum('cit,cjt->cij', rows_side[1], cols_side[1], preferred_element_...  9.05 us
    dot_general x9, matrix products, pair_tile(): jnp.einsum('cit,cjt->cij', rows_side[0], cols_side[0], preferred_element_...  8.85 us
    dot_general x9, matrix products, pair_tile(): jnp.einsum('cit,cjt->cij', rows_side[1], cols_side[0], preferred_element_...  8.8 us
    dot_general x9, matrix products, pair_tile(): jnp.einsum('cit,cjt->cij', rows_side[0], cols_side[1], preferred_element_...  7.76 us
    ppermute x4, starting transfers between devices, passed_along(): return lax.ppermute(block, axis, route)  5.24 us
  transfers between devices with their start and end apart: 5, of which 4 were waited for; matrix products, arithmetic and copies ran while one was open for 17% of the time, Pallas kernels for 0%

commit v1 on v0

--- a/solution.py
+++ b/solution.py
@@ -108,7 +108,12 @@
         second_block = (own_block + second_member) % NBLK
         tiles_list.append(jnp.where(first_block < second_block, product, flipped))
     tile_slots = jnp.stack(tiles_list, axis=2)
-    received = lax.all_to_all(tile_slots[:, None], "tile", split_axis=4, concat_axis=1, tiled=True)
+    received = jnp.concatenate(
+        lax.all_to_all(
+            jnp.stack(jnp.split(tile_slots[:, None], lax.axis_size("tile"), axis=4)), "tile", 0, 0
+        ),
+        axis=1,
+    )
     return channel_order(received, NBLK // 2 + 1, cover_sources(NBLK // 2 + 1, members))
 
 

time: 125 us -> 133 us (1.064)
  local copies, waits for them, and re-layouts: 4.71 us -> 12.9 us
    unnamed x10 -> x25, local copies, waits for them, and re-layouts: 0.02 us -> 9.63 us
    broadcast_in_dim x1 -> x0, local copies, waits for them, and re-layouts: 1.97 us -> none  [on_device(): tile_slots[:, None]]
  transfers between devices with their start and end apart: 5 -> 5, of which waited for: 4 -> 4; matrix products, arithmetic and copies ran while one was open for 17% -> 16% of each run, Pallas kernels for 0% -> 0%
where the time goes in v1:
time: 133 us; the launch traced here: 132 us
  waiting for transfers between devices  55 us (41%)
  matrix products  34.5 us (26%)
  starting transfers between devices  28.9 us (22%)
  local copies, waits for them, and re-layouts  12.9 us (10%)
    all_to_all x1, waiting for transfers between devices, on_device(): lax.all_to_all(jnp.stack(jnp.split(tile_slots[:, None], lax.axis_size('ti...  27.7 us
    ppermute x4, waiting for transfers between devices, passed_along(): return lax.ppermute(block, axis, route)  27.3 us
    all_to_all x1, starting transfers between devices, on_device(): lax.all_to_all(jnp.stack(jnp.split(tile_slots[:, None], lax.axis_size('ti...  23.7 us
    unnamed x25, local copies, waits for them, and re-layouts  9.63 us
    dot_general x9, matrix products, pair_tile(): jnp.einsum('cit,cjt->cij', rows_side[1], cols_side[1], preferred_element_...  9.05 us
    dot_general x9, matrix products, pair_tile(): jnp.einsum('cit,cjt->cij', rows_side[0], cols_side[0], preferred_element_...  8.85 us
    dot_general x9, matrix products, pair_tile(): jnp.einsum('cit,cjt->cij', rows_side[1], cols_side[0], preferred_element_...  8.8 us
    dot_general x9, matrix products, pair_tile(): jnp.einsum('cit,cjt->cij', rows_side[0], cols_side[1], preferred_element_...  7.76 us
  transfers between devices with their start and end apart: 5, of which 4 were waited for; matrix products, arithmetic and copies ran while one was open for 16% of the time, Pallas kernels for 0%

profile of v1, /device:TPU:15, one launch (start us, length us, event | category | flops | bytes accessed | tf_op | source)
XLA Modules:
  0.0 132.5 jit_solution(4183949672873392497)
XLA Ops:
  0.9 4.3 %collective-permute-start.2 = (bf16[2,1,128,1024]{3,2,1,0:T(8,128)(2,1)}, bf16[2,1,128,1024]{3,2,1,0:T(8,128)(2,1)}, u32[]{:S(2)}, u32[]{:S(2)}) collective-permute-start(bf16[2,1,128,1024]{3,2,1,0:T(8,128)(2,1)} %param.2), channel_id=1, source_target_pairs={{5,0},{6,1},{7,2},{8,3},{9,4},{10,5},{11,6},{12,7},{13,8},{14,9},{... | collective-permute-start | bytes 1572872 | tf_op jit(solution)/shard_map/ppermute | solution.py:14
  5.2 1.3 fusion.32
  6.5 1.3 fusion.1
  7.9 1.3 fusion.15
  9.4 5.8 %collective-permute-done = bf16[2,1,128,1024]{3,2,1,0:T(8,128)(2,1)S(1)} collective-permute-done((bf16[2,1,128,1024]{3,2,1,0:T(8,128)(2,1)}, bf16[2,1,128,1024]{3,2,1,0:T(8,128)(2,1)S(1)}, u32[]{:S(2)}, u32[]{:S(2)}) %collective-permute-start) | collective-permute-done | bytes 524320 | tf_op jit(solution)/shard_map/ppermute | solution.py:14
  16.3 2.3 %collective-permute-done.1 = bf16[2,1,128,1024]{3,2,1,0:T(8,128)(2,1)S(1)} collective-permute-done((bf16[2,1,128,1024]{3,2,1,0:T(8,128)(2,1)}, bf16[2,1,128,1024]{3,2,1,0:T(8,128)(2,1)S(1)}, u32[]{:S(2)}, u32[]{:S(2)}) %collective-permute-start.1) | collective-permute-done | bytes 524320 | tf_op jit(solution)/shard_map/ppermute | solution.py:14
  19.7 19.2 %collective-permute-done.2 = bf16[2,1,128,1024]{3,2,1,0:T(8,128)(2,1)} collective-permute-done((bf16[2,1,128,1024]{3,2,1,0:T(8,128)(2,1)}, bf16[2,1,128,1024]{3,2,1,0:T(8,128)(2,1)}, u32[]{:S(2)}, u32[]{:S(2)}) %collective-permute-start.2) | collective-permute-done | bytes 524320 | tf_op jit(solution)/shard_map/ppermute | solution.py:14
  40.1 1.2 fusion.50
  41.3 1.2 convolution_add_fusion.5
  42.5 1.2 convolution_subtract_fusion.5
  43.8 1.2 fusion.48
  45.0 1.2 fusion.46
  46.2 1.2 convolution_add_fusion.4
  47.4 1.2 convolution_subtract_fusion.4
  48.7 1.2 fusion.6
  49.9 1.2 fusion.21
  51.1 1.2 convolution_add_fusion.3
  52.3 1.2 convolution_subtract_fusion.3
  53.7 1.3 fusion.51
  55.0 1.2 fusion.49
  56.2 1.2 convolution_add_fusion.2
  57.4 1.2 convolution_subtract_fusion.2
  58.7 1.2 fusion.47
  59.9 1.2 fusion.45
  61.1 1.2 convolution_add_fusion.1
  62.3 1.2 convolution_subtract_fusion.1
  63.7 1.3 fusion.3
  65.0 1.2 fusion.18
  66.2 1.2 convolution_add_fusion
  67.4 1.2 convolution_subtract_fusion
  79.2 23.7 %all-to-all-start = ((f32[16,2,1,1,9,8,128]{6,5,4,1,3,2,0:T(8,128)}), f32[16,2,1,1,9,8,128]{6,5,4,1,3,2,0:T(8,128)S(1)}, u32[]{:S(2)}, u32[]{:S(2)}) async-start(f32[16,2,1,1,9,8,128]{6,5,4,1,3,2,0:T(8,128)} %fusion.53), calls=%async_computation | async-start | bytes 2359296 | tf_op jit(solution)/shard_map/all_to_all | solution.py:112
  102.9 27.7 %all-to-all-done = f32[16,2,1,1,9,8,128]{6,5,4,1,3,2,0:T(8,128)S(1)} async-done(((f32[16,2,1,1,9,8,128]{6,5,4,1,3,2,0:T(8,128)}), f32[16,2,1,1,9,8,128]{6,5,4,1,3,2,0:T(8,128)S(1)}, u32[]{:S(2)}, u32[]{:S(2)}) %all-to-all-start) | async-done | bytes 1179680 | tf_op jit(solution)/shard_map/all_to_all | solution.py:112
  (85 shorter events, 17.5 us)
Async XLA Ops:
  0.0 9.1 %copy-start.1 = (bf16[2,1,128,1024]{3,2,1,0:T(8,128)(2,1)S(1)}, bf16[2,1,128,1024]{3,2,1,0:T(8,128)(2,1)}, u32[]{:S(2)}) copy-start(bf16[2,1,128,1024]{3,2,1,0:T(8,128)(2,1)} %param.2) | copy-start | bytes 1572868
  0.0 15.2 %collective-permute-start = (bf16[2,1,128,1024]{3,2,1,0:T(8,128)(2,1)}, bf16[2,1,128,1024]{3,2,1,0:T(8,128)(2,1)S(1)}, u32[]{:S(2)}, u32[]{:S(2)}) collective-permute-start(bf16[2,1,128,1024]{3,2,1,0:T(8,128)(2,1)} %param.2), channel_id=1, source_target_pairs={{1,0},{2,1},{3,2},{4,3},{5,4},{6,5},{7,6},{8,7},{9,8},{10,9},{11,1... | collective-permute-start | bytes 1572872 | tf_op jit(solution)/shard_map/ppermute | solution.py:14
  0.7 17.9 %collective-permute-start.1 = (bf16[2,1,128,1024]{3,2,1,0:T(8,128)(2,1)}, bf16[2,1,128,1024]{3,2,1,0:T(8,128)(2,1)S(1)}, u32[]{:S(2)}, u32[]{:S(2)}) collective-permute-start(bf16[2,1,128,1024]{3,2,1,0:T(8,128)(2,1)} %param.2), channel_id=1, source_target_pairs={{2,0},{3,1},{4,2},{5,3},{6,4},{7,5},{8,6},{9,7},{10,8},{11,9},{12,... | collective-permute-start | bytes 1572872 | tf_op jit(solution)/shard_map/ppermute | solution.py:14
  0.9 38.0 %collective-permute-start.2 = (bf16[2,1,128,1024]{3,2,1,0:T(8,128)(2,1)}, bf16[2,1,128,1024]{3,2,1,0:T(8,128)(2,1)}, u32[]{:S(2)}, u32[]{:S(2)}) collective-permute-start(bf16[2,1,128,1024]{3,2,1,0:T(8,128)(2,1)} %param.2), channel_id=1, source_target_pairs={{5,0},{6,1},{7,2},{8,3},{9,4},{10,5},{11,6},{12,7},{13,8},{14,9},{... | collective-permute-start | bytes 1572872 | tf_op jit(solution)/shard_map/ppermute | solution.py:14
  5.2 48.4 %collective-permute-start.3 = (bf16[2,1,128,1024]{3,2,1,0:T(8,128)(2,1)}, bf16[2,1,128,1024]{3,2,1,0:T(8,128)(2,1)}, u32[]{:S(2)}, u32[]{:S(2)}) collective-permute-start(bf16[2,1,128,1024]{3,2,1,0:T(8,128)(2,1)} %param.2), channel_id=1, source_target_pairs={{8,0},{9,1},{10,2},{11,3},{12,4},{13,5},{14,6},{15,7},{0,8},{1,9},... | collective-permute-start | bytes 1572872 | tf_op jit(solution)/shard_map/ppermute | solution.py:14
  18.6 23.9 %copy-start.3 = (bf16[2,1,128,1024]{3,2,1,0:T(8,128)(2,1)}, bf16[2,1,128,1024]{3,2,1,0:T(8,128)(2,1)S(1)}, u32[]{:S(2)}) copy-start(bf16[2,1,128,1024]{3,2,1,0:T(8,128)(2,1)S(1)} %collective-permute-done.1) | copy-start | bytes 1572868
  53.6 1.4 %copy-start.4 = (bf16[2,1,128,1024]{3,2,1,0:T(8,128)(2,1)S(1)}, bf16[2,1,128,1024]{3,2,1,0:T(8,128)(2,1)}, u32[]{:S(2)}) copy-start(bf16[2,1,128,1024]{3,2,1,0:T(8,128)(2,1)} %copy-done.3) | copy-start | bytes 1572868
  63.6 1.4 %copy-start.2 = (bf16[2,1,128,1024]{3,2,1,0:T(8,128)(2,1)S(1)}, bf16[2,1,128,1024]{3,2,1,0:T(8,128)(2,1)}, u32[]{:S(2)}) copy-start(bf16[2,1,128,1024]{3,2,1,0:T(8,128)(2,1)} %param.2) | copy-start | bytes 1572868
  79.2 23.7 %copy-start = (s32[136]{0:T(256)S(1)}, s32[136]{0:T(256)}, u32[]{:S(2)}) copy-start(s32[136]{0:T(256)} %constant.111) | copy-start | bytes 1636
  79.2 51.4 %all-to-all-start = ((f32[16,2,1,1,9,8,128]{6,5,4,1,3,2,0:T(8,128)}), f32[16,2,1,1,9,8,128]{6,5,4,1,3,2,0:T(8,128)S(1)}, u32[]{:S(2)}, u32[]{:S(2)}) async-start(f32[16,2,1,1,9,8,128]{6,5,4,1,3,2,0:T(8,128)} %fusion.53), calls=%async_computation | async-start | bytes 2359296 | tf_op jit(solution)/shard_map/all_to_all | solution.py:112
